TPU v7x, 32 devices: a whole 2x2x4 slice. The times are simulated.
32 devices in a mesh: groups: 2 (over x), blk: 8 (over z, y), rows: 2 (over core).
Axes of the slice: x: 2, y: 2, z: 4, core: 2. Of those that a mesh axis runs over, the one named last changes fastest.
Arguments:
- features: bfloat16 [8, 16, 256, 512], P('groups', 'rows', 'blk'), parts along dimension 0, may hold values from -60 to 60
- gain_in: float32 [512], replicated, may hold values from 0.25 to 1.75
- shift_in: float32 [512], replicated, may hold values from -3 to 3
- conv_first: bfloat16 [3, 3, 512, 256], replicated, may hold values from -0.09375 to 0.09375
- bias_first: float32 [256], replicated, may hold values from -3 to 3
- short_weight: bfloat16 [512, 256], replicated, may hold values from -0.25 to 0.25
- short_bias: float32 [256], replicated, may hold values from -3 to 3
- gains_rest: float32 [5, 256], replicated, may hold values from 0.25 to 1.75
- shifts_rest: float32 [5, 256], replicated, may hold values from -3 to 3
- convs_rest: bfloat16 [5, 3, 3, 256, 256], replicated, may hold values from -0.125 to 0.125
- biases_rest: float32 [5, 256], replicated, may hold values from -3 to 3
Outputs:
- decoded: bfloat16 [8, 16, 256, 256], P('groups', 'rows', 'blk'), parts along dimension 0
There are 2 independent parts, one for each index of `groups`. A program takes and returns all parts, laid end to end along the dimension named above; an argument that names none is the same for every part. Nothing has to cross between parts.
All inputs are finite; a program needn't handle non-finite values.
Results may differ from a plain program's by a relative error of at most 0.0065.
Values may be sent and summed in bfloat16 or wider, within the bound.
A program may use at most 128 MiB of HBM per device.

v0:
```python
import jax
import jax.numpy as jnp
from jax import lax
from jax.sharding import PartitionSpec as P

GROUPS = 32
RESNETS = 3
EPS = 1e-06


def with_halo(block, sides, width, periodic):
    for axis, dim in sides:
        count = lax.axis_size(axis)
        forward = [(i, i + 1) for i in range(count - 1)]
        if periodic:
            forward.append((count - 1, 0))
        backward = [(target, source) for source, target in forward]
        low = lax.ppermute(
            lax.slice_in_dim(block, block.shape[dim] - width, None, axis=dim), axis, forward
        )
        high = lax.ppermute(lax.slice_in_dim(block, 0, width, axis=dim), axis, backward)
        block = jnp.concatenate([low, block, high], axis=dim)
    return block


def group_totals(values, groups):
    shaped = values.reshape(values.shape[0], -1, groups, values.shape[3] // groups)
    return jnp.sum(shaped, axis=(1, 3))


def per_channel(stat, channels):
    return jnp.repeat(stat, channels // stat.shape[1], axis=1)[:, None, None, :]


def norm_act(values, inner, gain, shift):
    channels = values.shape[3]
    count = (
        inner.shape[1]
        * inner.shape[2]
        * lax.axis_size("blk")
        * lax.axis_size("rows")
        * (channels // GROUPS)
    )
    total, square = lax.psum(
        (group_totals(inner, GROUPS), group_totals(inner * inner, GROUPS)), ("blk", "rows")
    )
    center = total / count
    spread = square / count - center * center
    scaled = (values - per_channel(center, channels)) * per_channel(
        lax.rsqrt(spread + EPS), channels
    ) * gain + shift
    return scaled * jax.nn.sigmoid(scaled)


def convolve(padded, weight, bias):
    height = padded.shape[1] - 2
    width = padded.shape[2] - 2
    inputs = weight.shape[2]
    total = jnp.zeros((padded.shape[0] * height * width, weight.shape[3]), jnp.float32)
    for shift_row in range(3):
        band = padded[:, shift_row : shift_row + height]
        stacked = jnp.concatenate(
            [band[:, :, shift_col : shift_col + width] for shift_col in range(3)], axis=3
        )
        total = total + jnp.dot(
            stacked.reshape(-1, 3 * inputs),
            weight[shift_row].reshape(3 * inputs, weight.shape[3]),
            preferred_element_type=jnp.float32,
        )
    return total.reshape(padded.shape[0], height, width, weight.shape[3]) + bias


def extend_once(field):
    tall = with_halo(field, (("rows", 1),), 1, False)
    return with_halo(tall, (("blk", 2),), 1, True)


def body(
    features,
    gain_in,
    shift_in,
    conv_first,
    bias_first,
    short_weight,
    short_bias,
    gains_rest,
    shifts_rest,
    convs_rest,
    biases_rest,
):
    stream = features
    for block in range(RESNETS):
        if block == 0:
            first = (gain_in, shift_in, conv_first, bias_first)
        else:
            first = (
                gains_rest[2 * block - 1],
                shifts_rest[2 * block - 1],
                convs_rest[2 * block - 1],
                biases_rest[2 * block - 1],
            )
        second = (
            gains_rest[2 * block],
            shifts_rest[2 * block],
            convs_rest[2 * block],
            biases_rest[2 * block],
        )
        source = stream.astype(jnp.float32)
        active = norm_act(source, source, first[0], first[1]).astype(jnp.bfloat16)
        inner = convolve(extend_once(active), first[2], first[3]).astype(jnp.bfloat16)
        middle = inner.astype(jnp.float32)
        active_two = norm_act(middle, middle, second[0], second[1]).astype(jnp.bfloat16)
        branch = convolve(extend_once(active_two), second[2], second[3])
        if block == 0:
            flat = stream.reshape(-1, stream.shape[3])
            skip = jnp.dot(flat, short_weight, preferred_element_type=jnp.float32) + short_bias
            skip = skip.reshape(
                stream.shape[0], stream.shape[1], stream.shape[2], short_weight.shape[1]
            )
        else:
            skip = stream.astype(jnp.float32)
        stream = (skip + branch).astype(jnp.bfloat16)
    return stream


def solution(mesh):
    placed = (P("groups", "rows", "blk", None), P(), P(), P(), P(), P(), P(), P(), P(), P(), P())
    return jax.shard_map(
        body,
        mesh=mesh,
        in_specs=placed,
        out_specs=P("groups", "rows", "blk", None),
        check_vma=False,
    )
```

profile of v0, /device:TPU:0, one launch (start us, length us, event | category | flops | bytes accessed | tf_op | source)
XLA Modules:
  0.0 329.6 jit_solution(16887478936183795066)
XLA Ops:
  2.0 35.0 %all-reduce.5 = (f32[4,32]{1,0:T(4,128)S(1)}, f32[4,32]{1,0:T(4,128)S(1)}) all-reduce(f32[4,32]{1,0:T(4,128)S(1)} %reduce_sum.127, f32[4,32]{1,0:T(4,128)S(1)} %reduce_sum.124), channel_id=1, replica_groups=mesh['groups'=2,'blk'=8,'rows'=2] {'blk','rows'}, use_global_device_ids=true, to_apply=%region_5.0 | all-reduce | flops 256 | bytes 2048 | tf_op jit(solution)/shard_map/psum | solution.py:44
  41.0 2.9 fusion.68
  44.0 2.6 fusion.67
  47.4 4.7 %collective-permute-start.3 = (bf16[4,10,1,512]{3,2,1,0:T(2,128)(2,1)S(1)}, bf16[4,10,1,512]{3,2,1,0:T(2,128)(2,1)}, u32[]{:S(2)}, u32[]{:S(2)}) collective-permute-start(bf16[4,10,1,512]{3,2,1,0:T(2,128)(2,1)S(1)} %get-tuple-element.65), channel_id=1, source_target_pairs={{2,0},{4,2},{6,4},{8,6},{10,8},{12,10},{14,12},{0,14},{3,1},{5,3},... | collective-permute-start | bytes 122888 | tf_op jit(solution)/shard_map/ppermute | solution.py:21
  52.2 3.3 %collective-permute-done.2 = bf16[4,10,1,512]{3,2,1,0:T(2,128)(2,1)} collective-permute-done((bf16[4,10,1,512]{3,2,1,0:T(2,128)(2,1)}, bf16[4,10,1,512]{3,2,1,0:T(2,128)(2,1)}, u32[]{:S(2)}, u32[]{:S(2)}) %collective-permute-start.2) | collective-permute-done | bytes 40992 | tf_op jit(solution)/shard_map/ppermute | solution.py:18
  66.4 33.6 %all-reduce.4 = (f32[4,32]{1,0:T(4,128)S(1)}, f32[4,32]{1,0:T(4,128)S(1)}) all-reduce(f32[4,32]{1,0:T(4,128)S(1)} %copy.38, f32[4,32]{1,0:T(4,128)S(1)} %copy.37), channel_id=1, replica_groups=mesh['groups'=2,'blk'=8,'rows'=2] {'blk','rows'}, use_global_device_ids=true, to_apply=%region_9.0 | all-reduce | flops 256 | bytes 2048 | tf_op jit(solution)/shard_map/psum | solution.py:44
  105.4 4.7 %collective-permute-start.7 = (bf16[4,10,1,256]{3,2,1,0:T(2,128)(2,1)S(1)}, bf16[4,10,1,256]{3,2,1,0:T(2,128)(2,1)S(1)}, u32[]{:S(2)}, u32[]{:S(2)}) collective-permute-start(bf16[4,10,1,256]{3,2,1,0:T(2,128)(2,1)S(1)} %get-tuple-element.120), channel_id=1, source_target_pairs={{2,0},{4,2},{6,4},{8,6},{10,8},{12,10},{14,12},{0,14},{3,1},{5,3},... | collective-permute-start | bytes 61448 | tf_op jit(solution)/shard_map/ppermute | solution.py:21
  118.1 3.0 convert_reduce_fusion.1
  121.3 32.5 %all-reduce.3 = (f32[4,32]{1,0:T(4,128)S(1)}, f32[4,32]{1,0:T(4,128)S(1)}) all-reduce(f32[4,32]{1,0:T(4,128)S(1)} %copy.42, f32[4,32]{1,0:T(4,128)S(1)} %copy.41), channel_id=1, replica_groups=mesh['groups'=2,'blk'=8,'rows'=2] {'blk','rows'}, use_global_device_ids=true, to_apply=%region_13.0 | all-reduce | flops 256 | bytes 2048 | tf_op jit(solution)/shard_map/psum | solution.py:44
  158.1 1.8 collective-permute-done.9
  160.0 4.7 %collective-permute-start.11 = (bf16[4,10,1,256]{3,2,1,0:T(2,128)(2,1)S(1)}, bf16[4,10,1,256]{3,2,1,0:T(2,128)(2,1)S(1)}, u32[]{:S(2)}, u32[]{:S(2)}) collective-permute-start(bf16[4,10,1,256]{3,2,1,0:T(2,128)(2,1)S(1)} %get-tuple-element.116), channel_id=1, source_target_pairs={{2,0},{4,2},{6,4},{8,6},{10,8},{12,10},{14,12},{0,14},{3,1},{5,3},... | collective-permute-start | bytes 61448 | tf_op jit(solution)/shard_map/ppermute | solution.py:21
  164.8 1.9 collective-permute-done.10
  174.9 32.5 %all-reduce.2 = (f32[4,32]{1,0:T(4,128)S(1)}, f32[4,32]{1,0:T(4,128)S(1)}) all-reduce(f32[4,32]{1,0:T(4,128)S(1)} %copy.45, f32[4,32]{1,0:T(4,128)S(1)} %copy.44), channel_id=1, replica_groups=mesh['groups'=2,'blk'=8,'rows'=2] {'blk','rows'}, use_global_device_ids=true, to_apply=%region_17.0 | all-reduce | flops 256 | bytes 2048 | tf_op jit(solution)/shard_map/psum | solution.py:44
  210.8 1.8 collective-permute-done.13
  212.8 4.7 %collective-permute-start.15 = (bf16[4,10,1,256]{3,2,1,0:T(2,128)(2,1)S(1)}, bf16[4,10,1,256]{3,2,1,0:T(2,128)(2,1)S(1)}, u32[]{:S(2)}, u32[]{:S(2)}) collective-permute-start(bf16[4,10,1,256]{3,2,1,0:T(2,128)(2,1)S(1)} %get-tuple-element.112), channel_id=1, source_target_pairs={{2,0},{4,2},{6,4},{8,6},{10,8},{12,10},{14,12},{0,14},{3,1},{5,3},... | collective-permute-start | bytes 61448 | tf_op jit(solution)/shard_map/ppermute | solution.py:21
  217.6 1.9 collective-permute-done.14
  227.9 32.5 %all-reduce.1 = (f32[4,32]{1,0:T(4,128)S(1)}, f32[4,32]{1,0:T(4,128)S(1)}) all-reduce(f32[4,32]{1,0:T(4,128)S(1)} %copy.48, f32[4,32]{1,0:T(4,128)S(1)} %copy.47), channel_id=1, replica_groups=mesh['groups'=2,'blk'=8,'rows'=2] {'blk','rows'}, use_global_device_ids=true, to_apply=%region_21.0 | all-reduce | flops 256 | bytes 2048 | tf_op jit(solution)/shard_map/psum | solution.py:44
  264.6 1.8 collective-permute-done.17
  266.6 4.7 %collective-permute-start.19 = (bf16[4,10,1,256]{3,2,1,0:T(2,128)(2,1)S(1)}, bf16[4,10,1,256]{3,2,1,0:T(2,128)(2,1)S(1)}, u32[]{:S(2)}, u32[]{:S(2)}) collective-permute-start(bf16[4,10,1,256]{3,2,1,0:T(2,128)(2,1)S(1)} %get-tuple-element.108), channel_id=1, source_target_pairs={{2,0},{4,2},{6,4},{8,6},{10,8},{12,10},{14,12},{0,14},{3,1},{5,3},... | collective-permute-start | bytes 61448 | tf_op jit(solution)/shard_map/ppermute | solution.py:21
  271.4 1.9 collective-permute-done.18
  279.3 32.5 %all-reduce = (f32[4,32]{1,0:T(4,128)S(1)}, f32[4,32]{1,0:T(4,128)S(1)}) all-reduce(f32[4,32]{1,0:T(4,128)S(1)} %copy.51, f32[4,32]{1,0:T(4,128)S(1)} %copy.50), channel_id=1, replica_groups=mesh['groups'=2,'blk'=8,'rows'=2] {'blk','rows'}, use_global_device_ids=true, to_apply=%region_25.26 | all-reduce | flops 256 | bytes 2048 | tf_op jit(solution)/shard_map/psum | solution.py:44
  315.2 1.8 collective-permute-done.21
  317.2 4.7 %collective-permute-start.23 = (bf16[4,10,1,256]{3,2,1,0:T(2,128)(2,1)S(1)}, bf16[4,10,1,256]{3,2,1,0:T(2,128)(2,1)S(1)}, u32[]{:S(2)}, u32[]{:S(2)}) collective-permute-start(bf16[4,10,1,256]{3,2,1,0:T(2,128)(2,1)S(1)} %get-tuple-element.104), channel_id=1, source_target_pairs={{2,0},{4,2},{6,4},{8,6},{10,8},{12,10},{14,12},{0,14},{3,1},{5,3},... | collective-permute-start | bytes 61448 | tf_op jit(solution)/shard_map/ppermute | solution.py:21
  321.9 2.0 collective-permute-done.22
  (225 shorter events, 74.8 us)
Async XLA Ops:
  38.2 8.4 %collective-permute-start = (bf16[4,1,32,512]{3,2,1,0:T(8,128)(2,1)S(1)}, bf16[4,1,32,512]{3,2,1,0:T(8,128)(2,1)S(1)}, u32[]{:S(2)}, u32[]{:S(2)}) collective-permute-start(bf16[4,1,32,512]{3,2,1,0:T(8,128)(2,1)S(1)} %get-tuple-element.69), channel_id=1, source_target_pairs={{0,1},{2,3},{4,5},{6,7},{8,9},{10,11},{12,13},{14,15},{16,17},{18,... | collective-permute-start | bytes 393224 | tf_op jit(solution)/shard_map/ppermute | solution.py:18
  39.7 6.9 %collective-permute-start.1 = (bf16[4,1,32,512]{3,2,1,0:T(8,128)(2,1)S(1)}, bf16[4,1,32,512]{3,2,1,0:T(8,128)(2,1)S(1)}, u32[]{:S(2)}, u32[]{:S(2)}) collective-permute-start(bf16[4,1,32,512]{3,2,1,0:T(8,128)(2,1)S(1)} %get-tuple-element.70), channel_id=1, source_target_pairs={{1,0},{3,2},{5,4},{7,6},{9,8},{11,10},{13,12},{15,14},{17,16},{19,... | collective-permute-start | bytes 393224 | tf_op jit(solution)/shard_map/ppermute | solution.py:21
  47.4 8.2 %collective-permute-start.2 = (bf16[4,10,1,512]{3,2,1,0:T(2,128)(2,1)}, bf16[4,10,1,512]{3,2,1,0:T(2,128)(2,1)}, u32[]{:S(2)}, u32[]{:S(2)}) collective-permute-start(bf16[4,10,1,512]{3,2,1,0:T(2,128)(2,1)} %get-tuple-element.64), channel_id=1, source_target_pairs={{0,2},{2,4},{4,6},{6,8},{8,10},{10,12},{12,14},{14,0},{1,3},{3,5},... | collective-permute-start | bytes 122888 | tf_op jit(solution)/shard_map/ppermute | solution.py:18
  47.4 8.2 %collective-permute-start.3 = (bf16[4,10,1,512]{3,2,1,0:T(2,128)(2,1)S(1)}, bf16[4,10,1,512]{3,2,1,0:T(2,128)(2,1)}, u32[]{:S(2)}, u32[]{:S(2)}) collective-permute-start(bf16[4,10,1,512]{3,2,1,0:T(2,128)(2,1)S(1)} %get-tuple-element.65), channel_id=1, source_target_pairs={{2,0},{4,2},{6,4},{8,6},{10,8},{12,10},{14,12},{0,14},{3,1},{5,3},... | collective-permute-start | bytes 122888 | tf_op jit(solution)/shard_map/ppermute | solution.py:21
  100.8 3.1 collective-permute-start.4
  102.1 3.1 collective-permute-start.5
  105.3 6.8 %collective-permute-start.6 = (bf16[4,10,1,256]{3,2,1,0:T(2,128)(2,1)S(1)}, bf16[4,10,1,256]{3,2,1,0:T(2,128)(2,1)S(1)}, u32[]{:S(2)}, u32[]{:S(2)}) collective-permute-start(bf16[4,10,1,256]{3,2,1,0:T(2,128)(2,1)S(1)} %get-tuple-element.119), channel_id=1, source_target_pairs={{0,2},{2,4},{4,6},{6,8},{8,10},{10,12},{12,14},{14,0},{1,3},{3,5},... | collective-permute-start | bytes 61448 | tf_op jit(solution)/shard_map/ppermute | solution.py:18
  105.4 6.7 %collective-permute-start.7 = (bf16[4,10,1,256]{3,2,1,0:T(2,128)(2,1)S(1)}, bf16[4,10,1,256]{3,2,1,0:T(2,128)(2,1)S(1)}, u32[]{:S(2)}, u32[]{:S(2)}) collective-permute-start(bf16[4,10,1,256]{3,2,1,0:T(2,128)(2,1)S(1)} %get-tuple-element.120), channel_id=1, source_target_pairs={{2,0},{4,2},{6,4},{8,6},{10,8},{12,10},{14,12},{0,14},{3,1},{5,3},... | collective-permute-start | bytes 61448 | tf_op jit(solution)/shard_map/ppermute | solution.py:21
  155.4 2.6 collective-permute-start.8
  156.7 3.1 collective-permute-start.9
  160.0 6.8 %collective-permute-start.10 = (bf16[4,10,1,256]{3,2,1,0:T(2,128)(2,1)S(1)}, bf16[4,10,1,256]{3,2,1,0:T(2,128)(2,1)S(1)}, u32[]{:S(2)}, u32[]{:S(2)}) collective-permute-start(bf16[4,10,1,256]{3,2,1,0:T(2,128)(2,1)S(1)} %get-tuple-element.115), channel_id=1, source_target_pairs={{0,2},{2,4},{4,6},{6,8},{8,10},{10,12},{12,14},{14,0},{1,3},{3,5},... | collective-permute-start | bytes 61448 | tf_op jit(solution)/shard_map/ppermute | solution.py:18
  160.0 6.7 %collective-permute-start.11 = (bf16[4,10,1,256]{3,2,1,0:T(2,128)(2,1)S(1)}, bf16[4,10,1,256]{3,2,1,0:T(2,128)(2,1)S(1)}, u32[]{:S(2)}, u32[]{:S(2)}) collective-permute-start(bf16[4,10,1,256]{3,2,1,0:T(2,128)(2,1)S(1)} %get-tuple-element.116), channel_id=1, source_target_pairs={{2,0},{4,2},{6,4},{8,6},{10,8},{12,10},{14,12},{0,14},{3,1},{5,3},... | collective-permute-start | bytes 61448 | tf_op jit(solution)/shard_map/ppermute | solution.py:21
  208.2 2.6 collective-permute-start.12
  209.5 3.1 collective-permute-start.13
  212.7 6.8 %collective-permute-start.14 = (bf16[4,10,1,256]{3,2,1,0:T(2,128)(2,1)S(1)}, bf16[4,10,1,256]{3,2,1,0:T(2,128)(2,1)S(1)}, u32[]{:S(2)}, u32[]{:S(2)}) collective-permute-start(bf16[4,10,1,256]{3,2,1,0:T(2,128)(2,1)S(1)} %get-tuple-element.111), channel_id=1, source_target_pairs={{0,2},{2,4},{4,6},{6,8},{8,10},{10,12},{12,14},{14,0},{1,3},{3,5},... | collective-permute-start | bytes 61448 | tf_op jit(solution)/shard_map/ppermute | solution.py:18
  212.8 6.7 %collective-permute-start.15 = (bf16[4,10,1,256]{3,2,1,0:T(2,128)(2,1)S(1)}, bf16[4,10,1,256]{3,2,1,0:T(2,128)(2,1)S(1)}, u32[]{:S(2)}, u32[]{:S(2)}) collective-permute-start(bf16[4,10,1,256]{3,2,1,0:T(2,128)(2,1)S(1)} %get-tuple-element.112), channel_id=1, source_target_pairs={{2,0},{4,2},{6,4},{8,6},{10,8},{12,10},{14,12},{0,14},{3,1},{5,3},... | collective-permute-start | bytes 61448 | tf_op jit(solution)/shard_map/ppermute | solution.py:21
  262.0 2.6 collective-permute-start.16
  263.3 3.1 collective-permute-start.17
  266.5 6.8 %collective-permute-start.18 = (bf16[4,10,1,256]{3,2,1,0:T(2,128)(2,1)S(1)}, bf16[4,10,1,256]{3,2,1,0:T(2,128)(2,1)S(1)}, u32[]{:S(2)}, u32[]{:S(2)}) collective-permute-start(bf16[4,10,1,256]{3,2,1,0:T(2,128)(2,1)S(1)} %get-tuple-element.107), channel_id=1, source_target_pairs={{0,2},{2,4},{4,6},{6,8},{8,10},{10,12},{12,14},{14,0},{1,3},{3,5},... | collective-permute-start | bytes 61448 | tf_op jit(solution)/shard_map/ppermute | solution.py:18
  266.6 6.7 %collective-permute-start.19 = (bf16[4,10,1,256]{3,2,1,0:T(2,128)(2,1)S(1)}, bf16[4,10,1,256]{3,2,1,0:T(2,128)(2,1)S(1)}, u32[]{:S(2)}, u32[]{:S(2)}) collective-permute-start(bf16[4,10,1,256]{3,2,1,0:T(2,128)(2,1)S(1)} %get-tuple-element.108), channel_id=1, source_target_pairs={{2,0},{4,2},{6,4},{8,6},{10,8},{12,10},{14,12},{0,14},{3,1},{5,3},... | collective-permute-start | bytes 61448 | tf_op jit(solution)/shard_map/ppermute | solution.py:21
  312.6 2.6 collective-permute-start.20
  313.9 3.1 collective-permute-start.21
  317.1 6.8 %collective-permute-start.22 = (bf16[4,10,1,256]{3,2,1,0:T(2,128)(2,1)S(1)}, bf16[4,10,1,256]{3,2,1,0:T(2,128)(2,1)S(1)}, u32[]{:S(2)}, u32[]{:S(2)}) collective-permute-start(bf16[4,10,1,256]{3,2,1,0:T(2,128)(2,1)S(1)} %get-tuple-element.103), channel_id=1, source_target_pairs={{0,2},{2,4},{4,6},{6,8},{8,10},{10,12},{12,14},{14,0},{1,3},{3,5},... | collective-permute-start | bytes 61448 | tf_op jit(solution)/shard_map/ppermute | solution.py:18
  317.2 6.7 %collective-permute-start.23 = (bf16[4,10,1,256]{3,2,1,0:T(2,128)(2,1)S(1)}, bf16[4,10,1,256]{3,2,1,0:T(2,128)(2,1)S(1)}, u32[]{:S(2)}, u32[]{:S(2)}) collective-permute-start(bf16[4,10,1,256]{3,2,1,0:T(2,128)(2,1)S(1)} %get-tuple-element.104), channel_id=1, source_target_pairs={{2,0},{4,2},{6,4},{8,6},{10,8},{12,10},{14,12},{0,14},{3,1},{5,3},... | collective-permute-start | bytes 61448 | tf_op jit(solution)/shard_map/ppermute | solution.py:21
  (31 other events, 347.8 us)
where the time goes:
time: 331 us; the launch traced here: 330 us
  blocking collectives  199 us (60%)
  starting transfers between devices  44.3 us (13%)
  local copies, waits for them, and re-layouts  31.8 us (10%)
  other arithmetic  21.7 us (7%)
  waiting for transfers between devices  19.8 us (6%)
  matrix products  12.2 us (4%)
    psum x6, blocking collectives, norm_act(): lax.psum((group_totals(inner, GROUPS), group_totals(inner * inner, GROUPS...  199 us
    ppermute x12, starting transfers between devices, with_halo(): lax.ppermute(lax.slice_in_dim(block, 0, width, axis=dim), axis, backward)  36 us
    dot_general x18, matrix products, convolve(): jnp.dot(stacked.reshape(-1, 3 * inputs), weight[shift_row].reshape(3 * in...  11.8 us
    ppermute x12, waiting for transfers between devices, with_halo(): lax.ppermute(lax.slice_in_dim(block, block.shape[dim] - width, None, axis...  11.1 us
    ppermute x12, waiting for transfers between devices, with_halo(): lax.ppermute(lax.slice_in_dim(block, 0, width, axis=dim), axis, backward)  8.75 us
    ppermute x12, starting transfers between devices, with_halo(): lax.ppermute(lax.slice_in_dim(block, block.shape[dim] - width, None, axis...  8.32 us
    reduce_sum x8, other arithmetic, group_totals(): return jnp.sum(shaped, axis=(1, 3))  7.68 us
    reshape x5, local copies, waits for them, and re-layouts, convolve(): return total.reshape(padded.shape[0], height, width, weight.shape[3]) + bias  7.09 us
  transfers between devices with their start and end apart: 24, of which 11 were waited for; matrix products, arithmetic and copies ran while one was open for 2% of the time, Pallas kernels for 0%

commit v1 on v0

--- a/solution.py
+++ b/solution.py
@@ -42,7 +42,7 @@
         * (channels // GROUPS)
     )
     total, square = lax.psum(
-        (group_totals(inner, GROUPS), group_totals(inner * inner, GROUPS)), ("blk", "rows")
+        lax.psum((group_totals(inner, GROUPS), group_totals(inner * inner, GROUPS)), "rows"), "blk"
     )
     center = total / count
     spread = square / count - center * center

time: 331 us -> 276 us (0.83)
  blocking collectives: 199 us -> 147 us
  local copies, waits for them, and re-layouts: 31.8 us -> 27.3 us
    psum x6, blocking collectives: 199 us -> 14.9 us  [norm_act(): lax.psum((group_totals(inner, GROUPS), group_totals(inner * inner, GROUPS...]
    psum x0 -> x6, blocking collectives: none -> 132 us  [norm_act(): lax.psum(lax.psum((group_totals(inner, GROUPS), group_totals(inner * inne...]
  transfers between devices with their start and end apart: 24 -> 24, of which waited for: 11 -> 11; matrix products, arithmetic and copies ran while one was open for 2% -> 3% of each run, Pallas kernels for 0% -> 0%
where the time goes in v1:
time: 276 us; the launch traced here: 274 us
  blocking collectives  147 us (53%)
  starting transfers between devices  44.3 us (16%)
  local copies, waits for them, and re-layouts  27.3 us (10%)
  other arithmetic  22.8 us (8%)
  waiting for transfers between devices  19.8 us (7%)
  matrix products  12.2 us (4%)
    psum x6, blocking collectives, norm_act(): lax.psum(lax.psum((group_totals(inner, GROUPS), group_totals(inner * inne...  132 us
    ppermute x12, starting transfers between devices, with_halo(): lax.ppermute(lax.slice_in_dim(block, 0, width, axis=dim), axis, backward)  36 us
    psum x6, blocking collectives, norm_act(): lax.psum((group_totals(inner, GROUPS), group_totals(inner * inner, GROUPS...  14.9 us
    dot_general x18, matrix products, convolve(): jnp.dot(stacked.reshape(-1, 3 * inputs), weight[shift_row].reshape(3 * in...  11.8 us
    ppermute x12, waiting for transfers between devices, with_halo(): lax.ppermute(lax.slice_in_dim(block, block.shape[dim] - width, None, axis...  11.1 us
    reduce_sum x8, other arithmetic, group_totals(): return jnp.sum(shaped, axis=(1, 3))  8.77 us
    ppermute x12, waiting for transfers between devices, with_halo(): lax.ppermute(lax.slice_in_dim(block, 0, width, axis=dim), axis, backward)  8.75 us
    ppermute x12, starting transfers between devices, with_halo(): lax.ppermute(lax.slice_in_dim(block, block.shape[dim] - width, None, axis...  8.32 us
  transfers between devices with their start and end apart: 24, of which 11 were waited for; matrix products, arithmetic and copies ran while one was open for 3% of the time, Pallas kernels for 0%

profile of v1, /device:TPU:0, one launch (start us, length us, event | category | flops | bytes accessed | tf_op | source)
XLA Modules:
  0.0 274.4 jit_solution(15798554053953337799)
XLA Ops:
  2.0 2.6 all-reduce.11
  4.7 23.0 %all-reduce.5 = (f32[4,32]{1,0:T(4,128)S(1)}, f32[4,32]{1,0:T(4,128)S(1)}) all-reduce(f32[4,32]{1,0:T(4,128)S(1)} %get-tuple-element.43, f32[4,32]{1,0:T(4,128)S(1)} %get-tuple-element.44), channel_id=1, replica_groups=mesh['groups'=2,'blk'=8,'rows'=2] {'blk'}, use_global_device_ids=true, to_apply=%region_7.0 | all-reduce | flops 256 | bytes 2048 | tf_op jit(solution)/shard_map/psum | solution.py:44
  31.7 3.0 %fusion.68 = (bf16[1,3,512,256]{3,2,1,0:T(8,128)(2,1)S(1)}, bf16[1,3,512,256]{3,2,1,0:T(8,128)(2,1)}, bf16[1,3,512,256]{3,2,1,0:T(8,128)(2,1)}) fusion(bf16[3,3,512,256]{3,2,1,0:T(8,128)(2,1)} %param.14), kind=kLoop, calls=%fused_computation.167 | loop fusion | bytes 4718592 | tf_op jit(solution)/shard_map/slice | solution.py:67
  34.7 2.6 fusion.67
  38.0 4.7 %collective-permute-start.3 = (bf16[4,10,1,512]{3,2,1,0:T(2,128)(2,1)S(1)}, bf16[4,10,1,512]{3,2,1,0:T(2,128)(2,1)}, u32[]{:S(2)}, u32[]{:S(2)}) collective-permute-start(bf16[4,10,1,512]{3,2,1,0:T(2,128)(2,1)S(1)} %get-tuple-element.77), channel_id=1, source_target_pairs={{2,0},{4,2},{6,4},{8,6},{10,8},{12,10},{14,12},{0,14},{3,1},{5,3},... | collective-permute-start | bytes 122888 | tf_op jit(solution)/shard_map/ppermute | solution.py:21
  42.8 3.3 %collective-permute-done.2 = bf16[4,10,1,512]{3,2,1,0:T(2,128)(2,1)} collective-permute-done((bf16[4,10,1,512]{3,2,1,0:T(2,128)(2,1)}, bf16[4,10,1,512]{3,2,1,0:T(2,128)(2,1)}, u32[]{:S(2)}, u32[]{:S(2)}) %collective-permute-start.2) | collective-permute-done | bytes 40992 | tf_op jit(solution)/shard_map/ppermute | solution.py:18
  57.0 2.5 all-reduce.10
  59.5 21.7 %all-reduce.4 = (f32[4,32]{1,0:T(4,128)S(1)}, f32[4,32]{1,0:T(4,128)S(1)}) all-reduce(f32[4,32]{1,0:T(4,128)S(1)} %get-tuple-element.41, f32[4,32]{1,0:T(4,128)S(1)} %get-tuple-element.42), channel_id=1, replica_groups=mesh['groups'=2,'blk'=8,'rows'=2] {'blk'}, use_global_device_ids=true, to_apply=%region_13.0 | all-reduce | flops 256 | bytes 2048 | tf_op jit(solution)/shard_map/psum | solution.py:44
  86.5 4.7 %collective-permute-start.7 = (bf16[4,10,1,256]{3,2,1,0:T(2,128)(2,1)S(1)}, bf16[4,10,1,256]{3,2,1,0:T(2,128)(2,1)S(1)}, u32[]{:S(2)}, u32[]{:S(2)}) collective-permute-start(bf16[4,10,1,256]{3,2,1,0:T(2,128)(2,1)S(1)} %get-tuple-element.132), channel_id=1, source_target_pairs={{2,0},{4,2},{6,4},{8,6},{10,8},{12,10},{14,12},{0,14},{3,1},{5,3},... | collective-permute-start | bytes 61448 | tf_op jit(solution)/shard_map/ppermute | solution.py:21
  99.3 3.0 %convert_reduce_fusion.1 = (f32[4,32]{0,1:T(8,128)S(1)}, f32[4,32]{0,1:T(8,128)S(1)}, bf16[4,256,32,8]{1,0,3,2:T(4,128)(2,1)}) fusion(f32[4,256,32,8]{1,0,3,2:T(4,128)} %reshape.214, f32[4,256,32,8]{1,0,3,2:T(4,128)} %reshape.215, f32[32,8]{1,0:T(8,128)S(1)} %add.329), kind=kLoop, calls=%fused_computation.59 | loop fusion | flops 1834752 | bytes 2623488 | tf_op jit(solution)/shard_map/reduce_sum | solution.py:28
  102.4 2.5 all-reduce.9
  104.9 21.8 %all-reduce.3 = (f32[4,32]{1,0:T(4,128)S(1)}, f32[4,32]{1,0:T(4,128)S(1)}) all-reduce(f32[4,32]{1,0:T(4,128)S(1)} %get-tuple-element.39, f32[4,32]{1,0:T(4,128)S(1)} %get-tuple-element.40), channel_id=1, replica_groups=mesh['groups'=2,'blk'=8,'rows'=2] {'blk'}, use_global_device_ids=true, to_apply=%region_19.0 | all-reduce | flops 256 | bytes 2048 | tf_op jit(solution)/shard_map/psum | solution.py:44
  133.0 4.7 %collective-permute-start.11 = (bf16[4,10,1,256]{3,2,1,0:T(2,128)(2,1)S(1)}, bf16[4,10,1,256]{3,2,1,0:T(2,128)(2,1)S(1)}, u32[]{:S(2)}, u32[]{:S(2)}) collective-permute-start(bf16[4,10,1,256]{3,2,1,0:T(2,128)(2,1)S(1)} %get-tuple-element.128), channel_id=1, source_target_pairs={{2,0},{4,2},{6,4},{8,6},{10,8},{12,10},{14,12},{0,14},{3,1},{5,3},... | collective-permute-start | bytes 61448 | tf_op jit(solution)/shard_map/ppermute | solution.py:21
  145.6 2.5 all-reduce.8
  148.1 21.8 %all-reduce.2 = (f32[4,32]{1,0:T(4,128)S(1)}, f32[4,32]{1,0:T(4,128)S(1)}) all-reduce(f32[4,32]{1,0:T(4,128)S(1)} %get-tuple-element.37, f32[4,32]{1,0:T(4,128)S(1)} %get-tuple-element.38), channel_id=1, replica_groups=mesh['groups'=2,'blk'=8,'rows'=2] {'blk'}, use_global_device_ids=true, to_apply=%region_25.0 | all-reduce | flops 256 | bytes 2048 | tf_op jit(solution)/shard_map/psum | solution.py:44
  175.3 4.7 %collective-permute-start.15 = (bf16[4,10,1,256]{3,2,1,0:T(2,128)(2,1)S(1)}, bf16[4,10,1,256]{3,2,1,0:T(2,128)(2,1)S(1)}, u32[]{:S(2)}, u32[]{:S(2)}) collective-permute-start(bf16[4,10,1,256]{3,2,1,0:T(2,128)(2,1)S(1)} %get-tuple-element.124), channel_id=1, source_target_pairs={{2,0},{4,2},{6,4},{8,6},{10,8},{12,10},{14,12},{0,14},{3,1},{5,3},... | collective-permute-start | bytes 61448 | tf_op jit(solution)/shard_map/ppermute | solution.py:21
  189.2 2.5 all-reduce.7
  191.6 21.8 %all-reduce.1 = (f32[4,32]{1,0:T(4,128)S(1)}, f32[4,32]{1,0:T(4,128)S(1)}) all-reduce(f32[4,32]{1,0:T(4,128)S(1)} %get-tuple-element.35, f32[4,32]{1,0:T(4,128)S(1)} %get-tuple-element.36), channel_id=1, replica_groups=mesh['groups'=2,'blk'=8,'rows'=2] {'blk'}, use_global_device_ids=true, to_apply=%region_31.0 | all-reduce | flops 256 | bytes 2048 | tf_op jit(solution)/shard_map/psum | solution.py:44
  219.7 4.7 %collective-permute-start.19 = (bf16[4,10,1,256]{3,2,1,0:T(2,128)(2,1)S(1)}, bf16[4,10,1,256]{3,2,1,0:T(2,128)(2,1)S(1)}, u32[]{:S(2)}, u32[]{:S(2)}) collective-permute-start(bf16[4,10,1,256]{3,2,1,0:T(2,128)(2,1)S(1)} %get-tuple-element.120), channel_id=1, source_target_pairs={{2,0},{4,2},{6,4},{8,6},{10,8},{12,10},{14,12},{0,14},{3,1},{5,3},... | collective-permute-start | bytes 61448 | tf_op jit(solution)/shard_map/ppermute | solution.py:21
  224.5 1.9 collective-permute-done.18
  232.4 2.5 all-reduce.6
  234.8 21.8 %all-reduce = (f32[4,32]{1,0:T(4,128)S(1)}, f32[4,32]{1,0:T(4,128)S(1)}) all-reduce(f32[4,32]{1,0:T(4,128)S(1)} %get-tuple-element.33, f32[4,32]{1,0:T(4,128)S(1)} %get-tuple-element.34), channel_id=1, replica_groups=mesh['groups'=2,'blk'=8,'rows'=2] {'blk'}, use_global_device_ids=true, to_apply=%region_37.38 | all-reduce | flops 256 | bytes 2048 | tf_op jit(solution)/shard_map/psum | solution.py:44
  262.0 4.7 %collective-permute-start.23 = (bf16[4,10,1,256]{3,2,1,0:T(2,128)(2,1)S(1)}, bf16[4,10,1,256]{3,2,1,0:T(2,128)(2,1)S(1)}, u32[]{:S(2)}, u32[]{:S(2)}) collective-permute-start(bf16[4,10,1,256]{3,2,1,0:T(2,128)(2,1)S(1)} %get-tuple-element.116), channel_id=1, source_target_pairs={{2,0},{4,2},{6,4},{8,6},{10,8},{12,10},{14,12},{0,14},{3,1},{5,3},... | collective-permute-start | bytes 61448 | tf_op jit(solution)/shard_map/ppermute | solution.py:21
  266.7 2.0 collective-permute-done.22
  (229 shorter events, 82.6 us)
Async XLA Ops:
  28.8 8.4 %collective-permute-start = (bf16[4,1,32,512]{3,2,1,0:T(8,128)(2,1)S(1)}, bf16[4,1,32,512]{3,2,1,0:T(8,128)(2,1)S(1)}, u32[]{:S(2)}, u32[]{:S(2)}) collective-permute-start(bf16[4,1,32,512]{3,2,1,0:T(8,128)(2,1)S(1)} %get-tuple-element.81), channel_id=1, source_target_pairs={{0,1},{2,3},{4,5},{6,7},{8,9},{10,11},{12,13},{14,15},{16,17},{18,... | collective-permute-start | bytes 393224 | tf_op jit(solution)/shard_map/ppermute | solution.py:18
  30.4 6.9 %collective-permute-start.1 = (bf16[4,1,32,512]{3,2,1,0:T(8,128)(2,1)S(1)}, bf16[4,1,32,512]{3,2,1,0:T(8,128)(2,1)S(1)}, u32[]{:S(2)}, u32[]{:S(2)}) collective-permute-start(bf16[4,1,32,512]{3,2,1,0:T(8,128)(2,1)S(1)} %get-tuple-element.82), channel_id=1, source_target_pairs={{1,0},{3,2},{5,4},{7,6},{9,8},{11,10},{13,12},{15,14},{17,16},{19,... | collective-permute-start | bytes 393224 | tf_op jit(solution)/shard_map/ppermute | solution.py:21
  38.0 8.2 %collective-permute-start.2 = (bf16[4,10,1,512]{3,2,1,0:T(2,128)(2,1)}, bf16[4,10,1,512]{3,2,1,0:T(2,128)(2,1)}, u32[]{:S(2)}, u32[]{:S(2)}) collective-permute-start(bf16[4,10,1,512]{3,2,1,0:T(2,128)(2,1)} %get-tuple-element.76), channel_id=1, source_target_pairs={{0,2},{2,4},{4,6},{6,8},{8,10},{10,12},{12,14},{14,0},{1,3},{3,5},... | collective-permute-start | bytes 122888 | tf_op jit(solution)/shard_map/ppermute | solution.py:18
  38.0 8.2 %collective-permute-start.3 = (bf16[4,10,1,512]{3,2,1,0:T(2,128)(2,1)S(1)}, bf16[4,10,1,512]{3,2,1,0:T(2,128)(2,1)}, u32[]{:S(2)}, u32[]{:S(2)}) collective-permute-start(bf16[4,10,1,512]{3,2,1,0:T(2,128)(2,1)S(1)} %get-tuple-element.77), channel_id=1, source_target_pairs={{2,0},{4,2},{6,4},{8,6},{10,8},{12,10},{14,12},{0,14},{3,1},{5,3},... | collective-permute-start | bytes 122888 | tf_op jit(solution)/shard_map/ppermute | solution.py:21
  81.9 3.1 %collective-permute-start.4 = (bf16[4,1,32,256]{3,2,1,0:T(8,128)(2,1)S(1)}, bf16[4,1,32,256]{3,2,1,0:T(8,128)(2,1)S(1)}, u32[]{:S(2)}, u32[]{:S(2)}) collective-permute-start(bf16[4,1,32,256]{3,2,1,0:T(8,128)(2,1)S(1)} %get-tuple-element.156), channel_id=1, source_target_pairs={{0,1},{2,3},{4,5},{6,7},{8,9},{10,11},{12,13},{14,15},{16,17},{18,... | collective-permute-start | bytes 196616 | tf_op jit(solution)/shard_map/ppermute | solution.py:18
  83.2 3.1 %collective-permute-start.5 = (bf16[4,1,32,256]{3,2,1,0:T(8,128)(2,1)S(1)}, bf16[4,1,32,256]{3,2,1,0:T(8,128)(2,1)S(1)}, u32[]{:S(2)}, u32[]{:S(2)}) collective-permute-start(bf16[4,1,32,256]{3,2,1,0:T(8,128)(2,1)S(1)} %get-tuple-element.157), channel_id=1, source_target_pairs={{1,0},{3,2},{5,4},{7,6},{9,8},{11,10},{13,12},{15,14},{17,16},{19,... | collective-permute-start | bytes 196616 | tf_op jit(solution)/shard_map/ppermute | solution.py:21
  86.5 6.8 %collective-permute-start.6 = (bf16[4,10,1,256]{3,2,1,0:T(2,128)(2,1)S(1)}, bf16[4,10,1,256]{3,2,1,0:T(2,128)(2,1)S(1)}, u32[]{:S(2)}, u32[]{:S(2)}) collective-permute-start(bf16[4,10,1,256]{3,2,1,0:T(2,128)(2,1)S(1)} %get-tuple-element.131), channel_id=1, source_target_pairs={{0,2},{2,4},{4,6},{6,8},{8,10},{10,12},{12,14},{14,0},{1,3},{3,5},... | collective-permute-start | bytes 61448 | tf_op jit(solution)/shard_map/ppermute | solution.py:18
  86.5 6.7 %collective-permute-start.7 = (bf16[4,10,1,256]{3,2,1,0:T(2,128)(2,1)S(1)}, bf16[4,10,1,256]{3,2,1,0:T(2,128)(2,1)S(1)}, u32[]{:S(2)}, u32[]{:S(2)}) collective-permute-start(bf16[4,10,1,256]{3,2,1,0:T(2,128)(2,1)S(1)} %get-tuple-element.132), channel_id=1, source_target_pairs={{2,0},{4,2},{6,4},{8,6},{10,8},{12,10},{14,12},{0,14},{3,1},{5,3},... | collective-permute-start | bytes 61448 | tf_op jit(solution)/shard_map/ppermute | solution.py:21
  128.4 2.6 collective-permute-start.8
  129.7 3.1 %collective-permute-start.9 = (bf16[4,1,32,256]{3,2,1,0:T(8,128)(2,1)S(1)}, bf16[4,1,32,256]{3,2,1,0:T(8,128)(2,1)S(1)}, u32[]{:S(2)}, u32[]{:S(2)}) collective-permute-start(bf16[4,1,32,256]{3,2,1,0:T(8,128)(2,1)S(1)} %get-tuple-element.152), channel_id=1, source_target_pairs={{1,0},{3,2},{5,4},{7,6},{9,8},{11,10},{13,12},{15,14},{17,16},{19,... | collective-permute-start | bytes 196616 | tf_op jit(solution)/shard_map/ppermute | solution.py:21
  132.9 6.8 %collective-permute-start.10 = (bf16[4,10,1,256]{3,2,1,0:T(2,128)(2,1)S(1)}, bf16[4,10,1,256]{3,2,1,0:T(2,128)(2,1)S(1)}, u32[]{:S(2)}, u32[]{:S(2)}) collective-permute-start(bf16[4,10,1,256]{3,2,1,0:T(2,128)(2,1)S(1)} %get-tuple-element.127), channel_id=1, source_target_pairs={{0,2},{2,4},{4,6},{6,8},{8,10},{10,12},{12,14},{14,0},{1,3},{3,5},... | collective-permute-start | bytes 61448 | tf_op jit(solution)/shard_map/ppermute | solution.py:18
  133.0 6.7 %collective-permute-start.11 = (bf16[4,10,1,256]{3,2,1,0:T(2,128)(2,1)S(1)}, bf16[4,10,1,256]{3,2,1,0:T(2,128)(2,1)S(1)}, u32[]{:S(2)}, u32[]{:S(2)}) collective-permute-start(bf16[4,10,1,256]{3,2,1,0:T(2,128)(2,1)S(1)} %get-tuple-element.128), channel_id=1, source_target_pairs={{2,0},{4,2},{6,4},{8,6},{10,8},{12,10},{14,12},{0,14},{3,1},{5,3},... | collective-permute-start | bytes 61448 | tf_op jit(solution)/shard_map/ppermute | solution.py:21
  170.7 2.6 collective-permute-start.12
  172.0 3.1 %collective-permute-start.13 = (bf16[4,1,32,256]{3,2,1,0:T(8,128)(2,1)S(1)}, bf16[4,1,32,256]{3,2,1,0:T(8,128)(2,1)S(1)}, u32[]{:S(2)}, u32[]{:S(2)}) collective-permute-start(bf16[4,1,32,256]{3,2,1,0:T(8,128)(2,1)S(1)} %get-tuple-element.147), channel_id=1, source_target_pairs={{1,0},{3,2},{5,4},{7,6},{9,8},{11,10},{13,12},{15,14},{17,16},{19,... | collective-permute-start | bytes 196616 | tf_op jit(solution)/shard_map/ppermute | solution.py:21
  175.2 6.8 %collective-permute-start.14 = (bf16[4,10,1,256]{3,2,1,0:T(2,128)(2,1)S(1)}, bf16[4,10,1,256]{3,2,1,0:T(2,128)(2,1)S(1)}, u32[]{:S(2)}, u32[]{:S(2)}) collective-permute-start(bf16[4,10,1,256]{3,2,1,0:T(2,128)(2,1)S(1)} %get-tuple-element.123), channel_id=1, source_target_pairs={{0,2},{2,4},{4,6},{6,8},{8,10},{10,12},{12,14},{14,0},{1,3},{3,5},... | collective-permute-start | bytes 61448 | tf_op jit(solution)/shard_map/ppermute | solution.py:18
  175.3 6.7 %collective-permute-start.15 = (bf16[4,10,1,256]{3,2,1,0:T(2,128)(2,1)S(1)}, bf16[4,10,1,256]{3,2,1,0:T(2,128)(2,1)S(1)}, u32[]{:S(2)}, u32[]{:S(2)}) collective-permute-start(bf16[4,10,1,256]{3,2,1,0:T(2,128)(2,1)S(1)} %get-tuple-element.124), channel_id=1, source_target_pairs={{2,0},{4,2},{6,4},{8,6},{10,8},{12,10},{14,12},{0,14},{3,1},{5,3},... | collective-permute-start | bytes 61448 | tf_op jit(solution)/shard_map/ppermute | solution.py:21
  215.1 2.6 collective-permute-start.16
  216.4 3.1 %collective-permute-start.17 = (bf16[4,1,32,256]{3,2,1,0:T(8,128)(2,1)S(1)}, bf16[4,1,32,256]{3,2,1,0:T(8,128)(2,1)S(1)}, u32[]{:S(2)}, u32[]{:S(2)}) collective-permute-start(bf16[4,1,32,256]{3,2,1,0:T(8,128)(2,1)S(1)} %get-tuple-element.142), channel_id=1, source_target_pairs={{1,0},{3,2},{5,4},{7,6},{9,8},{11,10},{13,12},{15,14},{17,16},{19,... | collective-permute-start | bytes 196616 | tf_op jit(solution)/shard_map/ppermute | solution.py:21
  219.6 6.8 %collective-permute-start.18 = (bf16[4,10,1,256]{3,2,1,0:T(2,128)(2,1)S(1)}, bf16[4,10,1,256]{3,2,1,0:T(2,128)(2,1)S(1)}, u32[]{:S(2)}, u32[]{:S(2)}) collective-permute-start(bf16[4,10,1,256]{3,2,1,0:T(2,128)(2,1)S(1)} %get-tuple-element.119), channel_id=1, source_target_pairs={{0,2},{2,4},{4,6},{6,8},{8,10},{10,12},{12,14},{14,0},{1,3},{3,5},... | collective-permute-start | bytes 61448 | tf_op jit(solution)/shard_map/ppermute | solution.py:18
  219.7 6.7 %collective-permute-start.19 = (bf16[4,10,1,256]{3,2,1,0:T(2,128)(2,1)S(1)}, bf16[4,10,1,256]{3,2,1,0:T(2,128)(2,1)S(1)}, u32[]{:S(2)}, u32[]{:S(2)}) collective-permute-start(bf16[4,10,1,256]{3,2,1,0:T(2,128)(2,1)S(1)} %get-tuple-element.120), channel_id=1, source_target_pairs={{2,0},{4,2},{6,4},{8,6},{10,8},{12,10},{14,12},{0,14},{3,1},{5,3},... | collective-permute-start | bytes 61448 | tf_op jit(solution)/shard_map/ppermute | solution.py:21
  257.4 2.6 collective-permute-start.20
  258.7 3.1 %collective-permute-start.21 = (bf16[4,1,32,256]{3,2,1,0:T(8,128)(2,1)S(1)}, bf16[4,1,32,256]{3,2,1,0:T(8,128)(2,1)S(1)}, u32[]{:S(2)}, u32[]{:S(2)}) collective-permute-start(bf16[4,1,32,256]{3,2,1,0:T(8,128)(2,1)S(1)} %get-tuple-element.137), channel_id=1, source_target_pairs={{1,0},{3,2},{5,4},{7,6},{9,8},{11,10},{13,12},{15,14},{17,16},{19,... | collective-permute-start | bytes 196616 | tf_op jit(solution)/shard_map/ppermute | solution.py:21
  262.0 6.8 %collective-permute-start.22 = (bf16[4,10,1,256]{3,2,1,0:T(2,128)(2,1)S(1)}, bf16[4,10,1,256]{3,2,1,0:T(2,128)(2,1)S(1)}, u32[]{:S(2)}, u32[]{:S(2)}) collective-permute-start(bf16[4,10,1,256]{3,2,1,0:T(2,128)(2,1)S(1)} %get-tuple-element.115), channel_id=1, source_target_pairs={{0,2},{2,4},{4,6},{6,8},{8,10},{10,12},{12,14},{14,0},{1,3},{3,5},... | collective-permute-start | bytes 61448 | tf_op jit(solution)/shard_map/ppermute | solution.py:18
  262.0 6.7 %collective-permute-start.23 = (bf16[4,10,1,256]{3,2,1,0:T(2,128)(2,1)S(1)}, bf16[4,10,1,256]{3,2,1,0:T(2,128)(2,1)S(1)}, u32[]{:S(2)}, u32[]{:S(2)}) collective-permute-start(bf16[4,10,1,256]{3,2,1,0:T(2,128)(2,1)S(1)} %get-tuple-element.116), channel_id=1, source_target_pairs={{2,0},{4,2},{6,4},{8,6},{10,8},{12,10},{14,12},{0,14},{3,1},{5,3},... | collective-permute-start | bytes 61448 | tf_op jit(solution)/shard_map/ppermute | solution.py:21
  (30 other events, 279.3 us)
